TPU v7x, 32 devices: a whole 2x2x4 slice. The times are simulated.
32 devices in a mesh: depth: 16 (over z, y, x), spec: 2 (over core).
Axes of the slice: x: 2, y: 2, z: 4, core: 2. Of those that a mesh axis runs over, the one named last changes fastest.
Arguments:
- emission: bfloat16 [512, 64, 2048], P('depth', 'spec'), may hold values from 0.099609375 to 2
- opacity: bfloat16 [512, 64, 2048], P('depth', 'spec'), may hold values from 0.29882812 to 3
- bin_extinction: float32 [64], P('spec'), may hold values from 0.1 to 30
- entry: int32 [2048], replicated, may hold values from 0 to 127
- exit_cell: int32 [2048], replicated, may hold values from 384 to 512
- response: float32 [3, 64], P(None, 'spec'), may hold values from 0.05 to 1
Outputs:
- nearer_slab_rgb: float32 [16, 3, 2048], P('depth')
- image: float32 [3, 2048], replicated
All inputs are finite; a program needn't handle non-finite values.
Results may differ from a plain program's by a relative error of at most 0.0003.
Values sent between devices are 32-bit elements; how exact they have to be, the bound alone decides.
A program may use at most 64 MiB of HBM per device.

v0:
```python
import jax
import jax.numpy as jnp
from jax import lax
from jax.sharding import PartitionSpec as P


def merge_slabs(earlier, later):
    return (earlier[0] + earlier[1] * later[0], earlier[1] * later[1])


def body(emission, opacity, bin_extinction, entry, exit_cell, response):
    cells = emission.shape[0]
    sections = lax.axis_size("depth")
    cell_step = 1.0 / (cells * sections)
    depth = lax.axis_index("depth") * cells + jnp.arange(cells, dtype=jnp.int32)
    inside = (depth[:, None] >= entry[None, :]) & (depth[:, None] < exit_cell[None, :])
    live = jnp.where(inside, 1.0, 0.0).astype(jnp.float32)
    tau = bin_extinction[None, :, None] * opacity.astype(jnp.float32) * live[:, None, :] * cell_step
    rows = jnp.arange(cells, dtype=jnp.int32)
    lower = jnp.where(rows[None, :] < rows[:, None], 1.0, 0.0).astype(jnp.float32)
    before = jnp.einsum("ij,jbr->ibr", lower, tau, precision=lax.Precision.HIGHEST)
    light = jnp.sum(
        emission.astype(jnp.float32) * live[:, None, :] * cell_step * jnp.exp(-before), axis=0
    )
    trans = jnp.exp(-jnp.sum(tau, axis=0))
    pieces = (
        lax.all_to_all(light[None], "depth", split_axis=2, concat_axis=0, tiled=True),
        lax.all_to_all(trans[None], "depth", split_axis=2, concat_axis=0, tiled=True),
    )
    totals = lax.associative_scan(merge_slabs, (pieces[0], pieces[1]), axis=0)
    lead_light = jnp.concatenate([jnp.zeros_like(pieces[0][:1]), totals[0][:-1]], axis=0)
    lead_trans = jnp.concatenate([jnp.ones_like(pieces[1][:1]), totals[1][:-1]], axis=0)
    moved_light = lax.all_to_all(lead_light, "depth", split_axis=0, concat_axis=2, tiled=True)
    moved_trans = lax.all_to_all(lead_trans, "depth", split_axis=0, concat_axis=2, tiled=True)
    nearer_radiance = moved_light[0]
    nearer_transparency = moved_trans[0]
    front_part = jnp.dot(response, nearer_radiance, precision=lax.Precision.HIGHEST)
    slab_portion = jnp.dot(response, nearer_transparency * light, precision=lax.Precision.HIGHEST)
    nearer_slab_rgb, slab_colour_rgb = lax.psum((front_part, slab_portion), "spec")
    image = lax.psum(slab_colour_rgb, "depth")
    return (nearer_slab_rgb[None], image)


def solution(mesh):
    placed = (
        P("depth", "spec", None),
        P("depth", "spec", None),
        P("spec"),
        P(),
        P(),
        P(None, "spec"),
    )
    return jax.shard_map(
        body, mesh=mesh, in_specs=placed, out_specs=(P("depth", None, None), P()), check_vma=False
    )
```

profile of v0, /device:TPU:0, one launch (start us, length us, event | category | flops | bytes accessed | tf_op | source)
XLA Modules:
  0.0 190.8 jit_solution(17573433646198136472)
XLA Ops:
  0.7 0.8 and_select_fusion
  1.5 5.9 %fusion = f32[32,2048]{1,0:T(8,128)S(1)} fusion(f32[32]{0:T(128)} %param.8, f32[32,2048]{1,0:T(8,128)S(1)} %and_select_fusion, bf16[32,32,2048]{2,1,0:T(8,128)(2,1)} %param.7), kind=kLoop, calls=%fused_computation.2 | loop fusion | flops 10420224 | bytes 4718720 | tf_op jit(solution)/shard_map/reduce_sum | solution.py:25
  7.4 0.6 copy.48
  8.0 0.5 broadcast.88
  8.5 9.3 %reduce = f32[2048,32]{1,0:T(8,128)S(1)} reduce(f32[2048,1,32]{2,1,0:T(1,128)S(1)} %bitcast.63, f32[]{:T(128)} %broadcast.88), dimensions={1}, to_apply=%bitcast.47.reduce_sub_computation | reduce | bytes 524292
  17.9 1.1 reshape.76
  19.0 8.3 %all-to-all-start.1 = ((f32[16,1,4096]{2,1,0:T(1,128)}), f32[16,1,4096]{2,1,0:T(1,128)S(1)}, u32[]{:S(2)}, u32[]{:S(2)}) async-start(f32[16,1,4096]{2,1,0:T(1,128)} %reshape.76), calls=%async_computation.1 | async-start | bytes 524288 | tf_op jit(solution)/shard_map/all_to_all | solution.py:28
  27.4 21.2 %multiply_reduce_fusion = f32[32,2048]{1,0:T(8,128)S(1)} fusion(bf16[32,32,2048]{2,1,0:T(8,128)(2,1)} %param.6, f32[32]{0:T(128)S(1)} %copy-done.1, f32[32,2048]{1,0:T(8,128)S(1)} %and_select_fusion, bf16[32,32,2048]{2,1,0:T(8,128)(2,1)} %param.7), kind=kOutput, calls=%fused_computation | convolution fusion | flops 826214400 | bytes 8913024 | tf_op jit(solution)/shard_map/ij,jbr->ibr/dot_general | solution.py:21
  48.6 0.6 copy.46
  49.2 9.6 %reduce.2 = f32[2048,32]{1,0:T(8,128)S(1)} reduce(f32[2048,1,32]{2,1,0:T(1,128)S(1)} %bitcast.66, f32[]{:T(128)} %broadcast.88), dimensions={1}, to_apply=%bitcast.45.reduce_sub_computation | reduce | bytes 524292
  58.8 1.2 reshape.74
  59.9 6.9 %all-to-all-start = ((f32[16,1,4096]{2,1,0:T(1,128)}), f32[16,1,4096]{2,1,0:T(1,128)S(1)}, u32[]{:S(2)}, u32[]{:S(2)}) async-start(f32[16,1,4096]{2,1,0:T(1,128)} %reshape.74), calls=%async_computation | async-start | bytes 524288 | tf_op jit(solution)/shard_map/all_to_all | solution.py:27
  66.8 1.3 reduce.1
  68.1 1.8 reshape.77
  69.9 0.6 copy.49
  70.9 5.3 %all-to-all-done = f32[16,1,4096]{2,1,0:T(1,128)S(1)} async-done(((f32[16,1,4096]{2,1,0:T(1,128)}), f32[16,1,4096]{2,1,0:T(1,128)S(1)}, u32[]{:S(2)}, u32[]{:S(2)}) %all-to-all-start) | async-done | bytes 262176 | tf_op jit(solution)/shard_map/all_to_all | solution.py:27
  76.2 1.3 reduce.3
  77.4 1.8 reshape.75
  79.3 0.3 copy.57
  80.7 0.1 slice.138
  80.8 0.1 slice.135
  80.9 0.1 slice.133
  81.0 0.1 slice.136
  81.5 0.4 pad.59
  81.9 0.4 pad.58
  82.4 0.4 pad.56
  82.8 0.4 pad.57
  83.4 0.2 pad.60
  83.7 0.2 pad.62
  83.9 0.2 pad.63
  84.1 0.2 pad.61
  84.5 0.2 pad.84
  84.8 0.2 pad.125
  85.2 0.7 concatenate.31.clone
  85.9 3.5 %all-to-all-start.3 = ((f32[16,32,128]{2,1,0:T(8,128)}), f32[16,32,128]{2,1,0:T(8,128)S(1)}, u32[]{:S(2)}, u32[]{:S(2)}) async-start(f32[16,32,128]{2,1,0:T(8,128)} %concatenate.31.clone), calls=%async_computation.3 | async-start | bytes 524288 | tf_op jit(solution)/shard_map/all_to_all | solution.py:34
  89.5 0.2 pad.82
  89.7 0.2 pad.124
  90.1 0.7 concatenate.29.clone
  90.8 7.8 %all-to-all-done.3 = f32[16,32,128]{2,1,0:T(8,128)S(1)} async-done(((f32[16,32,128]{2,1,0:T(8,128)}), f32[16,32,128]{2,1,0:T(8,128)S(1)}, u32[]{:S(2)}, u32[]{:S(2)}) %all-to-all-start.3) | async-done | bytes 262176 | tf_op jit(solution)/shard_map/all_to_all | solution.py:34
  98.7 3.5 %all-to-all-start.2 = ((f32[16,32,128]{2,1,0:T(8,128)}), f32[16,32,128]{2,1,0:T(8,128)S(1)}, u32[]{:S(2)}, u32[]{:S(2)}) async-start(f32[16,32,128]{2,1,0:T(8,128)} %concatenate.29.clone), calls=%async_computation.2 | async-start | bytes 524288 | tf_op jit(solution)/shard_map/all_to_all | solution.py:33
  102.2 0.2 copy.55
  102.4 9.0 %all-to-all-done.2 = f32[16,32,128]{2,1,0:T(8,128)S(1)} async-done(((f32[16,32,128]{2,1,0:T(8,128)}), f32[16,32,128]{2,1,0:T(8,128)S(1)}, u32[]{:S(2)}, u32[]{:S(2)}) %all-to-all-start.2) | async-done | bytes 262176 | tf_op jit(solution)/shard_map/all_to_all | solution.py:33
  111.4 0.2 copy.52
  111.5 0.3 convolution_bitcast_fusion
  111.9 0.3 convolution_bitcast_fusion.1
  112.2 3.6 %all-reduce.18 = (f32[1,3,2048]{2,1,0:T(4,128)S(1)}, f32[3,2048]{1,0:T(4,128)S(1)}) all-reduce(f32[1,3,2048]{2,1,0:T(4,128)S(1)} %convolution_bitcast_fusion.1, f32[3,2048]{1,0:T(4,128)S(1)} %convolution_bitcast_fusion), channel_id=1, replica_groups=mesh['depth'=16,'spec'=2] {'spec'}, use_global_device_ids=true, to_apply=%region_2.3 | all-reduce | flops 12288 | bytes 98304 | tf_op jit(solution)/shard_map/psum | solution.py:39
  115.8 0.6 copy.56
  116.5 74.4 %psum.23 = f32[3,2048]{1,0:T(4,128)} all-reduce(f32[3,2048]{1,0:T(4,128)S(1)} %get-tuple-element.13), channel_id=1, replica_groups=mesh['depth'=16,'spec'=2] {'depth'}, use_global_device_ids=true, to_apply=%region_4.5 | all-reduce | flops 6144 | bytes 49152 | tf_op jit(solution)/shard_map/psum | solution.py:40
  (45 shorter events, 2.2 us)
Async XLA Ops:
  0.6 110.9 %copy-start = (f32[3,32]{1,0:T(4,128)S(1)}, f32[3,32]{1,0:T(4,128)}, u32[]{:S(2)}) copy-start(f32[3,32]{1,0:T(4,128)} %param.11) | copy-start | bytes 1156
  1.5 25.9 %copy-start.1 = (f32[32]{0:T(128)S(1)}, f32[32]{0:T(128)}, u32[]{:S(2)}) copy-start(f32[32]{0:T(128)} %param.8) | copy-start | bytes 388
  19.0 40.9 %all-to-all-start.1 = ((f32[16,1,4096]{2,1,0:T(1,128)}), f32[16,1,4096]{2,1,0:T(1,128)S(1)}, u32[]{:S(2)}, u32[]{:S(2)}) async-start(f32[16,1,4096]{2,1,0:T(1,128)} %reshape.76), calls=%async_computation.1 | async-start | bytes 524288 | tf_op jit(solution)/shard_map/all_to_all | solution.py:28
  59.9 16.2 %all-to-all-start = ((f32[16,1,4096]{2,1,0:T(1,128)}), f32[16,1,4096]{2,1,0:T(1,128)S(1)}, u32[]{:S(2)}, u32[]{:S(2)}) async-start(f32[16,1,4096]{2,1,0:T(1,128)} %reshape.74), calls=%async_computation | async-start | bytes 524288 | tf_op jit(solution)/shard_map/all_to_all | solution.py:27
  85.9 12.8 %all-to-all-start.3 = ((f32[16,32,128]{2,1,0:T(8,128)}), f32[16,32,128]{2,1,0:T(8,128)S(1)}, u32[]{:S(2)}, u32[]{:S(2)}) async-start(f32[16,32,128]{2,1,0:T(8,128)} %concatenate.31.clone), calls=%async_computation.3 | async-start | bytes 524288 | tf_op jit(solution)/shard_map/all_to_all | solution.py:34
  98.7 12.7 %all-to-all-start.2 = ((f32[16,32,128]{2,1,0:T(8,128)}), f32[16,32,128]{2,1,0:T(8,128)S(1)}, u32[]{:S(2)}, u32[]{:S(2)}) async-start(f32[16,32,128]{2,1,0:T(8,128)} %concatenate.29.clone), calls=%async_computation.2 | async-start | bytes 524288 | tf_op jit(solution)/shard_map/all_to_all | solution.py:33
where the time goes:
time: 192 us; the launch traced here: 191 us
  blocking collectives  78 us (41%)
  other arithmetic  28.9 us (15%)
  starting transfers between devices  22.3 us (12%)
  waiting for transfers between devices  22.1 us (12%)
  matrix products  21.8 us (11%)
  local copies, waits for them, and re-layouts  16.5 us (9%)
    psum x1, blocking collectives, body(): image = lax.psum(slab_colour_rgb, 'depth')  74.4 us
    dot_general x1, matrix products, body(): jnp.einsum('ij,jbr->ibr', lower, tau, precision=lax.Precision.HIGHEST)  21.2 us
    unnamed x2, other arithmetic  18.9 us
    all_to_all x1, waiting for transfers between devices, body(): lax.all_to_all(lead_light, 'depth', split_axis=0, concat_axis=2, tiled=True)  8.99 us
    all_to_all x1, starting transfers between devices, body(): lax.all_to_all(trans[None], 'depth', split_axis=2, concat_axis=0, tiled=T...  8.35 us
    all_to_all x1, waiting for transfers between devices, body(): lax.all_to_all(lead_trans, 'depth', split_axis=0, concat_axis=2, tiled=True)  7.84 us
    unnamed x14, local copies, waits for them, and re-layouts  7.74 us
    all_to_all x1, starting transfers between devices, body(): lax.all_to_all(light[None], 'depth', split_axis=2, concat_axis=0, tiled=T...  6.9 us
  transfers between devices with their start and end apart: 4, of which 3 were waited for; matrix products, arithmetic and copies ran while one was open for 20% of the time, Pallas kernels for 0%

commit v1 on v0

--- a/solution.py
+++ b/solution.py
@@ -37,7 +37,7 @@
     front_part = jnp.dot(response, nearer_radiance, precision=lax.Precision.HIGHEST)
     slab_portion = jnp.dot(response, nearer_transparency * light, precision=lax.Precision.HIGHEST)
     nearer_slab_rgb, slab_colour_rgb = lax.psum((front_part, slab_portion), "spec")
-    image = lax.psum(slab_colour_rgb, "depth")
+    image = jnp.sum(lax.all_gather(slab_colour_rgb, "depth"), axis=0)
     return (nearer_slab_rgb[None], image)
 
 

time: 192 us -> 159 us (0.83)
  blocking collectives: 78 us -> 44.4 us
    psum x1 -> x0, blocking collectives: 74.4 us -> none  [body(): image = lax.psum(slab_colour_rgb, 'depth')]
    all_gather x0 -> x1, blocking collectives: none -> 40.8 us  [body(): image = jnp.sum(lax.all_gather(slab_colour_rgb, 'depth'), axis=0)]
  transfers between devices with their start and end apart: 4 -> 4, of which waited for: 3 -> 3; matrix products, arithmetic and copies ran while one was open for 20% -> 24% of each run, Pallas kernels for 0% -> 0%
where the time goes in v1:
time: 159 us; the launch traced here: 158 us
  blocking collectives  44.4 us (28%)
  other arithmetic  29.6 us (19%)
  starting transfers between devices  22.3 us (14%)
  waiting for transfers between devices  22.1 us (14%)
  matrix products  21.8 us (14%)
  local copies, waits for them, and re-layouts  16.5 us (10%)
    all_gather x1, blocking collectives, body(): image = jnp.sum(lax.all_gather(slab_colour_rgb, 'depth'), axis=0)  40.8 us
    dot_general x1, matrix products, body(): jnp.einsum('ij,jbr->ibr', lower, tau, precision=lax.Precision.HIGHEST)  21.2 us
    unnamed x2, other arithmetic  18.9 us
    all_to_all x1, waiting for transfers between devices, body(): lax.all_to_all(lead_light, 'depth', split_axis=0, concat_axis=2, tiled=True)  8.98 us
    all_to_all x1, starting transfers between devices, body(): lax.all_to_all(trans[None], 'depth', split_axis=2, concat_axis=0, tiled=T...  8.35 us
    all_to_all x1, waiting for transfers between devices, body(): lax.all_to_all(lead_trans, 'depth', split_axis=0, concat_axis=2, tiled=True)  7.82 us
    unnamed x14, local copies, waits for them, and re-layouts  7.74 us
    all_to_all x1, starting transfers between devices, body(): lax.all_to_all(light[None], 'depth', split_axis=2, concat_axis=0, tiled=T...  6.9 us
  transfers between devices with their start and end apart: 4, of which 3 were waited for; matrix products, arithmetic and copies ran while one was open for 24% of the time, Pallas kernels for 0%

profile of v1, /device:TPU:0, one launch (start us, length us, event | category | flops | bytes accessed | tf_op | source)
XLA Modules:
  0.0 157.9 jit_solution(4440362353049649587)
XLA Ops:
  0.7 0.8 and_select_fusion
  1.5 5.9 %fusion = f32[32,2048]{1,0:T(8,128)S(1)} fusion(f32[32]{0:T(128)} %param.8, f32[32,2048]{1,0:T(8,128)S(1)} %and_select_fusion, bf16[32,32,2048]{2,1,0:T(8,128)(2,1)} %param.7), kind=kLoop, calls=%fused_computation.2 | loop fusion | flops 10420224 | bytes 4718720 | tf_op jit(solution)/shard_map/reduce_sum | solution.py:25
  7.4 0.6 copy.48
  8.0 0.5 broadcast.88
  8.5 9.3 %reduce = f32[2048,32]{1,0:T(8,128)S(1)} reduce(f32[2048,1,32]{2,1,0:T(1,128)S(1)} %bitcast.65, f32[]{:T(128)} %broadcast.88), dimensions={1}, to_apply=%bitcast.49.reduce_sub_computation | reduce | bytes 524292
  17.9 1.1 reshape.76
  19.0 8.3 %all-to-all-start.1 = ((f32[16,1,4096]{2,1,0:T(1,128)}), f32[16,1,4096]{2,1,0:T(1,128)S(1)}, u32[]{:S(2)}, u32[]{:S(2)}) async-start(f32[16,1,4096]{2,1,0:T(1,128)} %reshape.76), calls=%async_computation.1 | async-start | bytes 524288 | tf_op jit(solution)/shard_map/all_to_all | solution.py:28
  27.4 21.2 %multiply_reduce_fusion = f32[32,2048]{1,0:T(8,128)S(1)} fusion(bf16[32,32,2048]{2,1,0:T(8,128)(2,1)} %param.6, f32[32]{0:T(128)S(1)} %copy-done.1, f32[32,2048]{1,0:T(8,128)S(1)} %and_select_fusion, bf16[32,32,2048]{2,1,0:T(8,128)(2,1)} %param.7), kind=kOutput, calls=%fused_computation | convolution fusion | flops 826214400 | bytes 8913024 | tf_op jit(solution)/shard_map/ij,jbr->ibr/dot_general | solution.py:21
  48.6 0.6 copy.46
  49.2 9.6 %reduce.2 = f32[2048,32]{1,0:T(8,128)S(1)} reduce(f32[2048,1,32]{2,1,0:T(1,128)S(1)} %bitcast.68, f32[]{:T(128)} %broadcast.88), dimensions={1}, to_apply=%bitcast.47.reduce_sub_computation | reduce | bytes 524292
  58.8 1.2 reshape.74
  59.9 6.9 %all-to-all-start = ((f32[16,1,4096]{2,1,0:T(1,128)}), f32[16,1,4096]{2,1,0:T(1,128)S(1)}, u32[]{:S(2)}, u32[]{:S(2)}) async-start(f32[16,1,4096]{2,1,0:T(1,128)} %reshape.74), calls=%async_computation | async-start | bytes 524288 | tf_op jit(solution)/shard_map/all_to_all | solution.py:27
  66.8 1.3 reduce.1
  68.1 1.8 %reshape.77 = f32[2048,1,32]{2,1,0:T(1,128)S(1)} reshape(f32[16,4096]{1,0:T(8,128)S(1)} %reduce.1) | data formatting | bytes 524288
  69.9 0.6 copy.49
  70.9 5.3 %all-to-all-done = f32[16,1,4096]{2,1,0:T(1,128)S(1)} async-done(((f32[16,1,4096]{2,1,0:T(1,128)}), f32[16,1,4096]{2,1,0:T(1,128)S(1)}, u32[]{:S(2)}, u32[]{:S(2)}) %all-to-all-start) | async-done | bytes 262176 | tf_op jit(solution)/shard_map/all_to_all | solution.py:27
  76.1 1.3 reduce.3
  77.4 1.8 %reshape.75 = f32[2048,1,32]{2,1,0:T(1,128)S(1)} reshape(f32[16,4096]{1,0:T(8,128)S(1)} %reduce.3) | data formatting | bytes 524288
  79.2 0.3 copy.57
  80.7 0.1 slice.138
  80.8 0.1 slice.135
  80.9 0.1 slice.133
  81.5 0.4 pad.59
  81.9 0.4 pad.58
  82.3 0.4 pad.56
  82.8 0.4 pad.57
  83.3 0.2 pad.60
  83.6 0.2 pad.62
  83.9 0.2 pad.63
  84.1 0.2 pad.61
  84.5 0.2 pad.84
  84.8 0.2 pad.125
  85.1 0.7 concatenate.31.clone
  85.9 3.5 %all-to-all-start.3 = ((f32[16,32,128]{2,1,0:T(8,128)}), f32[16,32,128]{2,1,0:T(8,128)S(1)}, u32[]{:S(2)}, u32[]{:S(2)}) async-start(f32[16,32,128]{2,1,0:T(8,128)} %concatenate.31.clone), calls=%async_computation.3 | async-start | bytes 524288 | tf_op jit(solution)/shard_map/all_to_all | solution.py:34
  89.5 0.2 pad.82
  89.7 0.2 pad.124
  90.1 0.7 concatenate.29.clone
  90.8 7.8 %all-to-all-done.3 = f32[16,32,128]{2,1,0:T(8,128)S(1)} async-done(((f32[16,32,128]{2,1,0:T(8,128)}), f32[16,32,128]{2,1,0:T(8,128)S(1)}, u32[]{:S(2)}, u32[]{:S(2)}) %all-to-all-start.3) | async-done | bytes 262176 | tf_op jit(solution)/shard_map/all_to_all | solution.py:34
  98.6 3.5 %all-to-all-start.2 = ((f32[16,32,128]{2,1,0:T(8,128)}), f32[16,32,128]{2,1,0:T(8,128)S(1)}, u32[]{:S(2)}, u32[]{:S(2)}) async-start(f32[16,32,128]{2,1,0:T(8,128)} %concatenate.29.clone), calls=%async_computation.2 | async-start | bytes 524288 | tf_op jit(solution)/shard_map/all_to_all | solution.py:33
  102.2 0.2 copy.55
  102.3 9.0 %all-to-all-done.2 = f32[16,32,128]{2,1,0:T(8,128)S(1)} async-done(((f32[16,32,128]{2,1,0:T(8,128)}), f32[16,32,128]{2,1,0:T(8,128)S(1)}, u32[]{:S(2)}, u32[]{:S(2)}) %all-to-all-start.2) | async-done | bytes 262176 | tf_op jit(solution)/shard_map/all_to_all | solution.py:33
  111.3 0.2 copy.52
  111.5 0.3 convolution_bitcast_fusion
  111.8 0.3 convolution_bitcast_fusion.1
  112.2 3.6 %all-reduce.18 = (f32[1,3,2048]{2,1,0:T(4,128)S(1)}, f32[1,3,2048]{2,1,0:T(4,128)S(1)}) all-reduce(f32[1,3,2048]{2,1,0:T(4,128)S(1)} %convolution_bitcast_fusion.1, f32[1,3,2048]{2,1,0:T(4,128)S(1)} %convolution_bitcast_fusion), channel_id=1, replica_groups=mesh['depth'=16,'spec'=2] {'spec'}, use_global_device_ids=true, to_apply=%region_2.3 | all-reduce | flops 12288 | bytes 98304 | tf_op jit(solution)/shard_map/psum | solution.py:39
  115.8 0.6 copy.56
  116.4 40.8 %all_gather.7 = f32[16,3,2048]{2,1,0:T(4,128)S(1)} all-gather(f32[1,3,2048]{2,1,0:T(4,128)S(1)} %get-tuple-element.13), channel_id=1, replica_groups=mesh['depth'=16,'spec'=2] {'depth'}, dimensions={0}, use_global_device_ids=true | all-gather | bytes 417792 | tf_op jit(solution)/shard_map/all_gather | solution.py:40
  157.2 0.7 reduce_sum.29
  (46 shorter events, 2.3 us)
Async XLA Ops:
  0.6 110.9 %copy-start = (f32[3,32]{1,0:T(4,128)S(1)}, f32[3,32]{1,0:T(4,128)}, u32[]{:S(2)}) copy-start(f32[3,32]{1,0:T(4,128)} %param.11) | copy-start | bytes 1156
  1.5 25.9 %copy-start.1 = (f32[32]{0:T(128)S(1)}, f32[32]{0:T(128)}, u32[]{:S(2)}) copy-start(f32[32]{0:T(128)} %param.8) | copy-start | bytes 388
  19.0 40.9 %all-to-all-start.1 = ((f32[16,1,4096]{2,1,0:T(1,128)}), f32[16,1,4096]{2,1,0:T(1,128)S(1)}, u32[]{:S(2)}, u32[]{:S(2)}) async-start(f32[16,1,4096]{2,1,0:T(1,128)} %reshape.76), calls=%async_computation.1 | async-start | bytes 524288 | tf_op jit(solution)/shard_map/all_to_all | solution.py:28
  59.9 16.2 %all-to-all-start = ((f32[16,1,4096]{2,1,0:T(1,128)}), f32[16,1,4096]{2,1,0:T(1,128)S(1)}, u32[]{:S(2)}, u32[]{:S(2)}) async-start(f32[16,1,4096]{2,1,0:T(1,128)} %reshape.74), calls=%async_computation | async-start | bytes 524288 | tf_op jit(solution)/shard_map/all_to_all | solution.py:27
  85.9 12.8 %all-to-all-start.3 = ((f32[16,32,128]{2,1,0:T(8,128)}), f32[16,32,128]{2,1,0:T(8,128)S(1)}, u32[]{:S(2)}, u32[]{:S(2)}) async-start(f32[16,32,128]{2,1,0:T(8,128)} %concatenate.31.clone), calls=%async_computation.3 | async-start | bytes 524288 | tf_op jit(solution)/shard_map/all_to_all | solution.py:34
  98.6 12.7 %all-to-all-start.2 = ((f32[16,32,128]{2,1,0:T(8,128)}), f32[16,32,128]{2,1,0:T(8,128)S(1)}, u32[]{:S(2)}, u32[]{:S(2)}) async-start(f32[16,32,128]{2,1,0:T(8,128)} %concatenate.29.clone), calls=%async_computation.2 | async-start | bytes 524288 | tf_op jit(solution)/shard_map/all_to_all | solution.py:33
